TPU v7x, 128 devices: a whole 4x4x4 slice. The times are simulated.
128 devices in a mesh: enc: 8 (over z, core), ctx: 16 (over y, x).
Axes of the slice: x: 4, y: 4, z: 4, core: 2. Of those that a mesh axis runs over, the one named last changes fastest.
Arguments:
- patches: bfloat16 [6144, 1280], P('enc'), may hold values from -17 to 17
- patch_image: int32 [6144], P('enc'), may hold values from 63 to 1535, as said below
- vit_gain: float32 [1280], replicated, may hold values from 0.1 to 1.9
- vit_qkv: bfloat16 [1280, 16, 240], P(None, 'ctx')
- vit_proj: bfloat16 [1280, 1280], P('ctx'), may hold values from -0.15625 to 0.15625
- merge_gain: float32 [1280], replicated, may hold values from 0.1 to 1.9
- merge_up: bfloat16 [5120, 5120], P(None, 'ctx'), may hold values from -0.078125 to 0.078125
- merge_down: bfloat16 [5120, 8192], P('ctx', 'enc'), may hold values from -0.078125 to 0.078125
- text_embed: bfloat16 [6144, 8192], P('ctx', 'enc'), may hold values from -17 to 17
- placeholder_unit: int32 [6144], replicated, may hold values from -1 to 1535, as said below
- doc_id: int32 [6144], replicated, may hold values from 0 to 31, never falling along the last dimension, each value on 1 to 3456 neighbouring positions
- dec_gain: float32 [8192], replicated, may hold values from 0.1 to 1.9
- dec_wq: bfloat16 [8192, 4096], P(None, 'enc')
- dec_wk: bfloat16 [8192, 1024], P(None, 'enc')
- dec_wv: bfloat16 [8192, 1024], P(None, 'enc'), may hold values from -0.0625 to 0.0625
Outputs:
- attended: bfloat16 [6144, 4096], P('ctx', 'enc')
Inputs may be any that keep to these rules, and one draw needn't show every extreme that they name: `patch_image`: the patches of an image are consecutive, start at a multiple of 4, number a multiple of 4 and at most 256, and lie within one aligned block of 768 patches; image numbers never fall and differ between images; in every such block some image has exactly 256 patches. `placeholder_unit`: -1 marks a text position. Every unit appears exactly once; the units of one image fill consecutive placeholders in their order; the placeholders of an aligned block of 384 positions are consecutive and number at most 192, and some block holds exactly 192. `doc_id`: document numbers never fall; a document has at most 3456 positions, and some document exactly 3456.
All inputs are finite; a program needn't handle non-finite values.
Results may differ from a plain program's by a relative error of at most 0.0085.
Values may be sent and summed in bfloat16 or wider, within the bound.
A program may use at most 128 MiB of HBM per device.

v0:
```python
import math
import jax
import jax.numpy as jnp
from jax import lax
from jax.sharding import PartitionSpec as P

HD = 128
QPK = 4
EPSILON = 1e-06
NEGATIVE = -1e30


def in_blocks(x, dim, size):
    dims = x.shape
    blocks = x.reshape(*dims[:dim], size, dims[dim] // size, *dims[dim + 1 :])
    return jnp.moveaxis(blocks, dim, 0)


def sent_and_summed(x, axis, dim):
    blocks = in_blocks(x, dim, lax.axis_size(axis))
    arrived = lax.all_to_all(blocks, axis, split_axis=0, concat_axis=0, tiled=True)
    return arrived.sum(axis=0)


def in_order(blocks, dim):
    dims = list(blocks.shape[1:])
    dims[dim] *= blocks.shape[0]
    return jnp.moveaxis(blocks, 0, dim).reshape(dims)


def sent_to_all(x, axis):
    size = lax.axis_size(axis)
    return lax.all_to_all(jnp.broadcast_to(x[None], (size, *x.shape)), axis, 0, 0, tiled=True)


def gathered_copies(x, axis, dim):
    return in_order(sent_to_all(x, axis), dim)


def of_everyone(x, axis):
    return sent_to_all(x, axis).sum(axis=0)


def in_one_piece(arrays, axis, dim, along):
    widths = [a.shape[along] for a in arrays]
    both = jnp.concatenate(arrays, axis=along)
    result = lax.all_gather(both, axis, axis=dim, tiled=True)
    return tuple(jnp.split(result, [sum(widths[:k]) for k in range(1, len(widths))], axis=along))


def layer_norm(values, scaling):
    widened = values.astype(jnp.float32)
    center = widened - jnp.mean(widened, axis=1, keepdims=True)
    spread = jnp.mean(center * center, axis=1, keepdims=True)
    return (center * lax.rsqrt(spread + EPSILON) * scaling).astype(jnp.bfloat16)


def image_attention(queries, keys_in, values_in, image_ids):
    head_count, row_count, head_width = queries.shape
    block_rows = math.gcd(row_count, 512)
    scaling = head_width ** (-0.5)

    def image_one_block(offset):
        query_block = lax.dynamic_slice_in_dim(queries, offset, block_rows, 1)
        block_ids = lax.dynamic_slice_in_dim(image_ids, offset, block_rows, 0)
        allowed = block_ids[:, None] == image_ids[None, :]
        scores = (
            jnp.einsum("hqd,hkd->hqk", query_block, keys_in, preferred_element_type=jnp.float32)
            * scaling
        )
        scores = jnp.where(allowed[None], scores, NEGATIVE)
        highest = jnp.max(scores, axis=2, keepdims=True)
        weights = jnp.exp(scores - highest)
        totals = jnp.sum(weights, axis=2, keepdims=True)
        mixture = jnp.einsum(
            "hqk,hkd->hqd",
            weights.astype(jnp.bfloat16),
            values_in,
            preferred_element_type=jnp.float32,
        )
        return (mixture / totals).astype(jnp.bfloat16)

    offsets = jnp.arange(row_count // block_rows, dtype=jnp.int32) * block_rows
    blocks = lax.map(image_one_block, offsets)
    return blocks.transpose(1, 0, 2, 3).reshape(head_count, row_count, head_width)


def body(
    patches,
    patch_image,
    vit_gain,
    vit_qkv,
    vit_proj,
    merge_gain,
    merge_up,
    merge_down,
    text_embed,
    placeholder_unit,
    doc_id,
    dec_gain,
    dec_wq,
    dec_wk,
    dec_wv,
):
    ctx_count = lax.axis_size("ctx")
    enc_count = lax.axis_size("enc")
    ctx_index = lax.axis_index("ctx")
    group_rows = patches.shape[0]
    head_count = vit_qkv.shape[1]
    head_width = vit_qkv.shape[2] // 3
    normed_patches = layer_norm(patches, vit_gain)
    packed = jnp.dot(
        normed_patches,
        vit_qkv.reshape(vit_qkv.shape[0], head_count * 3 * head_width),
        preferred_element_type=jnp.float32,
    )
    packed = (
        packed.astype(jnp.bfloat16)
        .reshape(group_rows, head_count, 3, head_width)
        .transpose(2, 1, 0, 3)
    )
    attended_patches = image_attention(packed[0], packed[1], packed[2], patch_image)
    flat_heads = attended_patches.transpose(1, 0, 2).reshape(group_rows, head_count * head_width)
    head_terms = jnp.dot(flat_heads, vit_proj, preferred_element_type=jnp.float32)
    share_sum = sent_and_summed(head_terms, "ctx", 0)
    share_count = share_sum.shape[0]
    own_rows = lax.dynamic_slice_in_dim(patches, ctx_index * share_count, share_count, 0)
    own_out = (own_rows.astype(jnp.float32) + share_sum).astype(jnp.bfloat16)
    own_normed = layer_norm(lax.optimization_barrier(own_out), merge_gain)
    merge_input = gathered_copies(own_normed, "ctx", 0)
    unit_inputs = merge_input.reshape(group_rows // 4, 4 * merge_input.shape[1])
    hidden = jax.nn.gelu(
        jnp.dot(unit_inputs, merge_up, preferred_element_type=jnp.float32), approximate=False
    ).astype(jnp.bfloat16)
    all_hidden = gathered_copies(hidden, "enc", 0)
    unit_total = all_hidden.shape[0]
    tok_rows = text_embed.shape[0]
    feature_cols = text_embed.shape[1]
    local_units = lax.dynamic_slice_in_dim(placeholder_unit, ctx_index * tok_rows, tok_rows, 0)
    present = local_units >= 0
    slot_rows = tok_rows // 2
    shard_units = placeholder_unit.reshape(ctx_count, tok_rows)
    shard_present = shard_units >= 0
    shard_rank = jnp.cumsum(shard_present.astype(jnp.int32), axis=1) - 1
    matches = shard_present[:, None, :] & (
        shard_rank[:, None, :] == jnp.arange(slot_rows, dtype=jnp.int32)[None, :, None]
    )
    slot_units = (jnp.sum(jnp.where(matches, shard_units[:, None, :] + 1, 0), axis=2) - 1).reshape(
        -1
    )
    picked = jnp.take(all_hidden, jnp.clip(slot_units, 0, unit_total - 1), axis=0)
    picked = jnp.where((slot_units >= 0)[:, None], picked, jnp.zeros_like(picked))
    arrived = lax.psum_scatter(
        jnp.dot(picked, merge_down, preferred_element_type=jnp.float32),
        "ctx",
        scatter_dimension=0,
        tiled=True,
    ).astype(jnp.bfloat16)
    local_rank = jnp.cumsum(present.astype(jnp.int32)) - 1
    vision_local = jnp.take(arrived, jnp.clip(local_rank, 0, slot_rows - 1), axis=0)
    sequence = jnp.where(present[:, None], vision_local, text_embed)
    local_wide = sequence.astype(jnp.float32)
    squares = of_everyone(jnp.sum(local_wide * local_wide, axis=1), "enc")
    row_scale = lax.rsqrt(squares / (feature_cols * enc_count) + EPSILON)
    start_state = (
        jnp.zeros((tok_rows, dec_wq.shape[1]), jnp.float32),
        jnp.zeros((tok_rows, dec_wk.shape[1]), jnp.float32),
        jnp.zeros((tok_rows, dec_wv.shape[1]), jnp.float32),
    )
    normed_part = (
        lax.all_gather(sequence, "enc", axis=1, tiled=True).astype(jnp.float32)
        * row_scale[:, None]
        * dec_gain
    ).astype(jnp.bfloat16)
    query_part = jnp.dot(normed_part, dec_wq, preferred_element_type=jnp.float32)
    key_part = jnp.dot(normed_part, dec_wk, preferred_element_type=jnp.float32)
    value_part = jnp.dot(normed_part, dec_wv, preferred_element_type=jnp.float32)
    queries_flat = query_part.astype(jnp.bfloat16)
    keys_local = key_part.astype(jnp.bfloat16)
    values_local = value_part.astype(jnp.bfloat16)
    kv_local = dec_wk.shape[1] // HD
    queries = queries_flat.reshape(tok_rows, kv_local, QPK, HD).transpose(1, 2, 0, 3)
    query_first = ctx_index * tok_rows
    query_pos = query_first + jnp.arange(tok_rows, dtype=jnp.int32)
    query_docs = lax.dynamic_slice_in_dim(doc_id, query_first, tok_rows, 0)
    scaling = HD ** (-0.5)
    start_state = (
        jnp.full((kv_local, QPK, tok_rows), NEGATIVE, jnp.float32),
        jnp.zeros((kv_local, QPK, tok_rows), jnp.float32),
        jnp.zeros((kv_local, QPK, tok_rows, HD), jnp.float32),
    )
    offset = jnp.int32(0)
    key_part, value_part = in_one_piece((keys_local, values_local), "ctx", 0, 1)
    key_count = key_part.shape[0]
    sub_rows = math.gcd(key_count, 512)
    last_doc = lax.dynamic_slice_in_dim(doc_id, offset + key_count - 1, 1, 0)[0]
    visible = (offset <= query_first + tok_rows - 1) & (last_doc >= query_docs[0])

    def update(current):

        def update_one_block(turn_index, inner_state):
            highest, totals, mixture = inner_state
            begin_row = turn_index * sub_rows
            keys_block = lax.dynamic_slice_in_dim(key_part, begin_row, sub_rows, 0).reshape(
                sub_rows, kv_local, HD
            )
            values_block = lax.dynamic_slice_in_dim(value_part, begin_row, sub_rows, 0).reshape(
                sub_rows, kv_local, HD
            )
            key_pos = begin_row + jnp.arange(sub_rows, dtype=jnp.int32)
            key_docs = lax.dynamic_slice_in_dim(doc_id, begin_row, sub_rows, 0)
            allowed = (key_pos[None, :] <= query_pos[:, None]) & (
                key_docs[None, :] == query_docs[:, None]
            )
            scores = (
                jnp.einsum(
                    "gjtd,sgd->gjts", queries, keys_block, preferred_element_type=jnp.float32
                )
                * scaling
            )
            new_peak = jnp.maximum(highest, jnp.max(jnp.where(allowed, scores, NEGATIVE), axis=3))
            factor = jnp.exp(highest - new_peak)
            weights = jnp.where(allowed, jnp.exp(scores - new_peak[..., None]), 0.0)
            totals = totals * factor + jnp.sum(weights, axis=3)
            mixture = mixture * factor[..., None] + jnp.einsum(
                "gjts,sgd->gjtd",
                weights.astype(jnp.bfloat16),
                values_block,
                preferred_element_type=jnp.float32,
            )
            return (new_peak, totals, mixture)

        return lax.fori_loop(0, key_count // sub_rows, update_one_block, current)

    def unchanged(current):
        return current

    finished = lax.cond(visible, update, unchanged, start_state)
    outputs = (finished[2] / finished[1][..., None]).astype(jnp.bfloat16)
    return outputs.transpose(2, 0, 1, 3).reshape(tok_rows, kv_local * QPK * HD)


def solution(mesh):
    placed = (
        P("enc", None),
        P("enc"),
        P(),
        P(None, "ctx", None),
        P("ctx", None),
        P(),
        P(None, "ctx"),
        P("ctx", "enc"),
        P("ctx", "enc"),
        P(),
        P(),
        P(),
        P(None, "enc"),
        P(None, "enc"),
        P(None, "enc"),
    )
    return jax.shard_map(
        body, mesh=mesh, in_specs=placed, out_specs=P("ctx", "enc"), check_vma=False
    )
```

profile of v0, /device:TPU:0, one launch (start us, length us, event | category | flops | bytes accessed | tf_op | source)
XLA Modules:
  0.0 493.8 jit_solution(5505292122462072174)
XLA Ops:
  6.6 2.0 convert_reduce_fusion
  11.3 2.0 copy.40
  13.3 1.9 slice_bitcast_fusion
  15.2 16.2 %while.28 = (s32[]{:T(128)}, bf16[3,1,256,80]{2,3,1,0:T(8,128)(2,1)}, s32[3]{0:T(128)S(1)}, s32[768]{0:T(1024)S(1)}, bf16[1,768,80]{2,1,0:T(8,128)(2,1)}, /*inde...) while((s32[]{:T(128)}, ...), condition=%wide.region_10.11_spmd, body=%wide.region_7.10_spmd.sunk | while | flops 64527876 | bytes 2797211 | solution.py:84
  32.5 3.5 fusion.79
  36.0 7.2 %all-to-all-start = ((f32[16,48,1280]{2,1,0:T(8,128)}), f32[16,48,1280]{2,1,0:T(8,128)}, u32[]{:S(2)}, u32[]{:S(2)}) async-start(f32[16,48,1280]{2,1,0:T(8,128)} %fusion.79), calls=%async_computation | async-start | bytes 7864320 | tf_op jit(solution)/shard_map/all_to_all | solution.py:21
  43.2 59.5 %all-to-all-done = f32[16,48,1280]{2,1,0:T(8,128)} async-done(((f32[16,48,1280]{2,1,0:T(8,128)}), f32[16,48,1280]{2,1,0:T(8,128)}, u32[]{:S(2)}, u32[]{:S(2)}) %all-to-all-start) | async-done | bytes 3932192 | tf_op jit(solution)/shard_map/all_to_all | solution.py:21
  102.7 2.3 reduce_sum.97
  107.9 4.5 all-to-all-start.1
  115.6 24.9 %all-to-all-done.1 = bf16[16,48,1280]{2,1,0:T(8,128)(2,1)} async-done(((bf16[16,48,1280]{2,1,0:T(8,128)(2,1)}), bf16[16,48,1280]{2,1,0:T(8,128)(2,1)}, u32[]{:S(2)}, u32[]{:S(2)}) %all-to-all-start.1) | async-done | bytes 1966112 | tf_op jit(solution)/shard_map/all_to_all | solution.py:33
  140.5 4.1 reshape_reshape.3
  144.6 3.6 fusion.66
  149.3 5.3 %all-to-all-start.2 = ((bf16[8,192,320]{2,1,0:T(8,128)(2,1)}), bf16[8,192,320]{2,1,0:T(8,128)(2,1)S(1)}, u32[]{:S(2)}, u32[]{:S(2)}) async-start(bf16[8,192,320]{2,1,0:T(8,128)(2,1)} %broadcast_in_dim.158), calls=%async_computation.2 | async-start | bytes 2359296 | tf_op jit(solution)/shard_map/all_to_all | solution.py:33
  154.7 17.3 %all-to-all-done.2 = bf16[8,192,320]{2,1,0:T(8,128)(2,1)S(1)} async-done(((bf16[8,192,320]{2,1,0:T(8,128)(2,1)}), bf16[8,192,320]{2,1,0:T(8,128)(2,1)S(1)}, u32[]{:S(2)}, u32[]{:S(2)}) %all-to-all-start.2) | async-done | bytes 983072 | tf_op jit(solution)/shard_map/all_to_all | solution.py:33
  171.9 11.0 %gather_fusion = bf16[3072,320]{1,0:T(8,128)(2,1)S(1)} fusion(bf16[1536,320]{1,0:T(8,128)(2,1)S(1)} %bitcast.146, s32[3072]{0:T(1024)S(1)} %broadcast_clamp_fusion), kind=kCustom, calls=%fused_computation | custom fusion | bytes 3944448 | tf_op jit(solution)/shard_map/jit(_take)/gather | solution.py:151
  182.9 7.6 %fusion.47 = f32[3072,1024]{1,0:T(8,128)} fusion(bf16[320,1024]{1,0:T(8,128)(2,1)} %param.28, bf16[3072,320]{1,0:T(8,128)(2,1)S(1)} %gather_fusion, pred[3072]{0:T(1024)(128)(4,1)} %compare_and_fusion.1, pred[3072]{0:T(1024)(128)(4,1)S(1)} %ge.77), kind=kOutput, calls=%fused_computation.61 | convolution fusion | flops 2015232000 | bytes 15210496 | tf_op jit(solution)/shard_map/dot_general | solution.py:154
  192.2 88.8 %reduce-scatter.2.cloned.1.call-done = f32[192,1024]{1,0:T(8,128)} async-done(((f32[3072,1024]{1,0:T(8,128)}), f32[192,1024]{1,0:T(8,128)}) %reduce-scatter.2.cloned.1.call-update) | async-done | bytes 786448 | tf_op jit(solution)/shard_map/reduce_scatter | solution.py:153
  282.2 2.1 gather_fusion.1
  285.7 9.6 %all_to_all.21 = f32[8,1,384]{2,1,0:T(1,128)S(1)} all-to-all(f32[8,1,384]{2,1,0:T(1,128)S(1)} %broadcast_in_dim.162), channel_id=1, replica_groups=mesh['enc'=8,'ctx'=16] {'enc'}, dimensions={0} | all-to-all | bytes 24576 | tf_op jit(solution)/shard_map/all_to_all | solution.py:33
  295.3 30.6 %all-gather.3.cloned.1.call-done = bf16[384,8192]{1,0:T(8,128)(2,1)} async-done(((bf16[384,1024]{1,0:T(8,128)(2,1)}), bf16[384,8192]{1,0:T(8,128)(2,1)}) %all-gather.3.cloned.1.call-update) | async-done | bytes 6291472 | tf_op jit(solution)/shard_map/all_gather | solution.py:171
  325.9 5.7 %convolution_convert_fusion.2 = bf16[384,128]{0,1:T(8,128)(2,1)S(1)} fusion(bf16[8192,128]{1,0:T(8,128)(2,1)} %param.34, bf16[384,8192]{1,0:T(8,128)(2,1)} %all-gather.3.cloned.1.call-done, f32[8192]{0:T(1024)S(1)} %copy-done.10, f32[384]{0:T(512)S(1)} %add_rsqrt_fusion.1), kind=kOutput, calls=%fused_computation.76 | convolution fusion | flops 817938432 | bytes 8521216 | tf_op jit(solution)/shard_map/dot_general | solution.py:176
  331.7 2.2 convolution_convert_fusion.1
  338.5 8.7 %convolution_convert_fusion = bf16[384,512]{1,0:T(8,128)(2,1)S(1)} fusion(bf16[8192,512]{1,0:T(8,128)(2,1)} %param.33, bf16[384,8192]{1,0:T(8,128)(2,1)} %all-gather.3.cloned.1.call-done, f32[8192]{0:T(1024)S(1)} %copy-done.10, f32[384]{0:T(512)S(1)} %add_rsqrt_fusion.1), kind=kOutput, calls=%fused_computation.71 | convolution fusion | flops 3234004992 | bytes 15107584 | tf_op jit(solution)/shard_map/dot_general | solution.py:175
  348.1 38.2 %all-gather.5.cloned.1.call-done = bf16[6144,256]{0,1:T(8,128)(2,1)} async-done(((bf16[384,256]{0,1:T(8,128)(2,1)}), bf16[6144,256]{0,1:T(8,128)(2,1)}) %all-gather.5.cloned.1.call-update) | async-done | bytes 3145744 | tf_op jit(solution)/shard_map/all_gather | solution.py:47
  386.4 98.2 %conditional.1 = (f32[1,4,384]{2,1,0:T(4,128)}, f32[1,4,384,128]{3,2,1,0:T(8,128)}) conditional(s32[]{:T(128)} %convert_element_type.75, () %tuple.31, (bf16[6144,256]{0,1:T(8,128)(2,1)}, s32[]{:T(128)}, s32[384]{0:T(512)S(1)}, s32[6144]{0:T(1024)}, s32[384]{0:T(512)S(1)}, /*index=5*/bf16[1,4,384,128]{3,2,1,0:T(8,128)(2,1)}) %tuple.87), branch_computations={%region_17.18_spmd, %region_18.23_spmd} | conditional | flops 412493696 | bytes 25149788 | solution.py:238
  386.4 3.2 copy.44
  389.5 1.9 fusion.87
  391.4 93.2 %while.27 = (s32[]{:T(128)}, f32[1,4,384]{2,1,0:T(4,128)S(1)}, f32[1,4,384]{2,1,0:T(4,128)}, f32[1,4,384,128]{3,2,1,0:T(8,128)}, s32[384]{0:T(512)S(1)}, /*index...) while((s32[]{:T(128)}, f32[1,4,384]{2,1,0:T(4,128)S(1)}, ...), condition=%wide.region_22.22_spmd.clone, body=%wide.region_19.21_spmd.clone.sunk | while | flops 412493312 | bytes 12563663 | solution.py:233
  394.2 2.8 fusion.116
  401.0 3.1 fusion.116
  408.9 3.1 fusion.116
  416.7 3.1 fusion.116
  422.8 1.7 fusion.113
  424.6 3.1 fusion.116
  430.6 1.7 fusion.113
  432.4 3.1 fusion.116
  438.5 1.7 fusion.113
  440.3 3.1 fusion.116
  446.3 1.7 fusion.113
  448.1 3.1 fusion.116
  454.2 1.7 fusion.113
  456.0 3.1 fusion.116
  462.0 1.7 fusion.113
  463.8 3.1 fusion.116
  469.9 1.7 fusion.113
  471.7 3.1 fusion.116
  477.7 1.7 fusion.113
  479.5 3.1 fusion.116
  (195 shorter events, 73.9 us)
Async XLA Ops:
  6.5 138.1 %copy-start = (bf16[5120,320]{0,1:T(8,128)(2,1)S(1)}, bf16[5120,320]{0,1:T(8,128)(2,1)}, u32[]{:S(2)}) copy-start(bf16[5120,320]{0,1:T(8,128)(2,1)} %param.27) | copy-start | bytes 9830404
  6.5 3.0 copy-start.11
  6.5 2.3 copy-start.2
  6.5 3.0 copy-start.9
  9.5 5.7 %copy-start.6 = (s32[768]{0:T(1024)S(1)}, s32[768]{0:T(1024)}, u32[]{:S(2)}) copy-start(s32[768]{0:T(1024)} %param.22) | copy-start | bytes 9220
  36.0 66.7 %all-to-all-start = ((f32[16,48,1280]{2,1,0:T(8,128)}), f32[16,48,1280]{2,1,0:T(8,128)}, u32[]{:S(2)}, u32[]{:S(2)}) async-start(f32[16,48,1280]{2,1,0:T(8,128)} %fusion.79), calls=%async_computation | async-start | bytes 7864320 | tf_op jit(solution)/shard_map/all_to_all | solution.py:21
  43.2 63.2 %copy-start.5 = (f32[1280]{0:T(1024)S(1)}, f32[1280]{0:T(1024)}, u32[]{:S(2)}) copy-start(f32[1280]{0:T(1024)} %param.26) | copy-start | bytes 15364
  106.3 6.0 %copy-start.4 = (s32[6144]{0:T(1024)S(1)}, s32[6144]{0:T(1024)}, u32[]{:S(2)}) copy-start(s32[6144]{0:T(1024)} %param.30) | copy-start | bytes 73732
  107.9 32.7 %all-to-all-start.1 = ((bf16[16,48,1280]{2,1,0:T(8,128)(2,1)}), bf16[16,48,1280]{2,1,0:T(8,128)(2,1)}, u32[]{:S(2)}, u32[]{:S(2)}) async-start(bf16[16,48,1280]{2,1,0:T(8,128)(2,1)} %broadcast_in_dim.157), calls=%async_computation.1 | async-start | bytes 3932160 | tf_op jit(solution)/shard_map/all_to_all | solution.py:33
  149.3 22.6 %all-to-all-start.2 = ((bf16[8,192,320]{2,1,0:T(8,128)(2,1)}), bf16[8,192,320]{2,1,0:T(8,128)(2,1)S(1)}, u32[]{:S(2)}, u32[]{:S(2)}) async-start(bf16[8,192,320]{2,1,0:T(8,128)(2,1)} %broadcast_in_dim.158), calls=%async_computation.2 | async-start | bytes 2359296 | tf_op jit(solution)/shard_map/all_to_all | solution.py:33
  154.6 126.4 %reduce-scatter.2.cloned.1.call-start = ((), (), s32[]{:S(2)}) async-start(), calls=%async_computation.5 | async-start | bytes 13369344 | tf_op jit(solution)/shard_map/reduce_scatter | solution.py:153
  190.6 135.3 %all-gather.3.cloned.1.call-start = ((), (), s32[]{:S(2)}) async-start(), calls=%async_computation.6 | async-start | bytes 7077888 | tf_op jit(solution)/shard_map/all_gather | solution.py:171
  282.1 2.1 copy-start.3
  284.2 41.7 %copy-start.10 = (f32[8192]{0:T(1024)S(1)}, f32[8192]{0:T(1024)}, u32[]{:S(2)}) copy-start(f32[8192]{0:T(1024)} %param.32) | copy-start | bytes 98308
  285.6 100.7 %all-gather.5.cloned.1.call-start = ((), (), s32[]{:S(2)}) async-start(), calls=%async_computation.7 | async-start | bytes 3342336 | tf_op jit(solution)/shard_map/all_gather | solution.py:47
  295.3 36.3 %copy-start.8 = (bf16[8192,128]{1,0:T(8,128)(2,1)S(1)}, bf16[8192,128]{1,0:T(8,128)(2,1)}, u32[]{:S(2)}) copy-start(bf16[8192,128]{1,0:T(8,128)(2,1)} %param.35) | copy-start | bytes 6291460
  325.9 5.7 %copy-start.7 = (bf16[384,8192]{1,0:T(8,128)(2,1)S(1)}, bf16[384,8192]{1,0:T(8,128)(2,1)}, u32[]{:S(2)}) copy-start(bf16[384,8192]{1,0:T(8,128)(2,1)} %all-gather.3.cloned.1.call-done) | copy-start | bytes 18874372
  484.6 2.7 copy-start.1
Sparse Core Ops, SparseCore 0:
  190.7 90.2 reduce-scatter.1
  285.8 40.1 all-gather.2
  334.7 51.5 all-gather.4
where the time goes:
time: 496 us; the launch traced here: 494 us
  waiting for transfers between devices  259 us (52%)
  matrix products  97.8 us (20%)
  local copies, waits for them, and re-layouts  46.6 us (9%)
  other arithmetic  41.9 us (8%)
  starting transfers between devices  17.1 us (3%)
  between operations  14.8 us (3%)
  blocking collectives  9.58 us (2%)
  loops' own time  6.57 us (1%)
    reduce_scatter x1, waiting for transfers between devices, body(): lax.psum_scatter(jnp.dot(picked, merge_down, preferred_element_type=jnp.f...  88.8 us
    all_to_all x1, waiting for transfers between devices, sent_and_summed(): lax.all_to_all(blocks, axis, split_axis=0, concat_axis=0, tiled=True)  59.5 us
    all_to_all x2, waiting for transfers between devices, sent_to_all(): lax.all_to_all(jnp.broadcast_to(x[None], (size, *x.shape)), axis, 0, 0, t...  42.2 us
    all_gather x1, waiting for transfers between devices, in_one_piece(): result = lax.all_gather(both, axis, axis=dim, tiled=True)  38.2 us
    dot_general x12, matrix products, update_one_block(): jnp.einsum('gjts,sgd->gjtd', weights.astype(jnp.bfloat16), values_block,...  36.9 us
    all_gather x1, waiting for transfers between devices, body(): lax.all_gather(sequence, 'enc', axis=1, tiled=True).astype(jnp.float32)  30.6 us
    dot_general x12, matrix products, update_one_block(): jnp.einsum('gjtd,sgd->gjts', queries, keys_block, preferred_element_type=...  20.9 us
    add x12, other arithmetic, update_one_block(): totals = totals * factor + jnp.sum(weights, axis=3)  14.8 us
  transfers between devices with their start and end apart: 6, of which 6 were waited for; matrix products, arithmetic and copies ran while one was open for 3% of the time, Pallas kernels for 0%

commit v1 on v0

--- a/solution.py
+++ b/solution.py
@@ -102,6 +102,17 @@
     dec_wk,
     dec_wv,
 ):
+
+    def drive_the_gates(along_axis, frame_in):
+        n_shards = lax.axis_size(along_axis)
+        store = []
+        for kk in tuple(range(frame_in.ndim)):
+            store.append(n_shards if kk == 1 else 1)
+        carry_in = lax.all_to_all(
+            jnp.tile(frame_in, store), tiled=True, split_axis=1, axis_name=along_axis, concat_axis=1
+        )
+        return carry_in
+
     ctx_count = lax.axis_size("ctx")
     enc_count = lax.axis_size("enc")
     ctx_index = lax.axis_index("ctx")
@@ -168,9 +179,7 @@
         jnp.zeros((tok_rows, dec_wv.shape[1]), jnp.float32),
     )
     normed_part = (
-        lax.all_gather(sequence, "enc", axis=1, tiled=True).astype(jnp.float32)
-        * row_scale[:, None]
-        * dec_gain
+        drive_the_gates("enc", sequence).astype(jnp.float32) * row_scale[:, None] * dec_gain
     ).astype(jnp.bfloat16)
     query_part = jnp.dot(normed_part, dec_wq, preferred_element_type=jnp.float32)
     key_part = jnp.dot(normed_part, dec_wk, preferred_element_type=jnp.float32)

time: 496 us -> 553 us (1.11)
  waiting for transfers between devices: 259 us -> 298 us
  local copies, waits for them, and re-layouts: 46.6 us -> 60.5 us
    all_to_all x0 -> x1, waiting for transfers between devices: none -> 72 us  [drive_the_gates(): lax.all_to_all(jnp.tile(frame_in, store), tiled=True, split_axis=1, axis_...]
    all_gather x1 -> x0, waiting for transfers between devices: 30.6 us -> none  [body(): lax.all_gather(sequence, 'enc', axis=1, tiled=True).astype(jnp.float32)]
    all_to_all x0 -> x1, local copies, waits for them, and re-layouts: none -> 8.63 us  [drive_the_gates(): lax.all_to_all(jnp.tile(frame_in, store), tiled=True, split_axis=1, axis_...]
    convert_element_type x0 -> x1, other arithmetic: none -> 5.61 us  [body(): normed_part = (drive_the_gates('enc', sequence).astype(jnp.float32) * row...]
where the time goes in v1:
time: 553 us; the launch traced here: 551 us
  waiting for transfers between devices  298 us (54%)
  matrix products  92.7 us (17%)
  local copies, waits for them, and re-layouts  60.5 us (11%)
  other arithmetic  46.7 us (8%)
  starting transfers between devices  21.8 us (4%)
  between operations  15.1 us (3%)
  blocking collectives  9.58 us (2%)
  loops' own time  6.57 us (1%)
    reduce_scatter x1, waiting for transfers between devices, body(): lax.psum_scatter(jnp.dot(picked, merge_down, preferred_element_type=jnp.f...  88.8 us
    all_to_all x1, waiting for transfers between devices, drive_the_gates(): lax.all_to_all(jnp.tile(frame_in, store), tiled=True, split_axis=1, axis_...  72 us
    all_to_all x1, waiting for transfers between devices, sent_and_summed(): lax.all_to_all(blocks, axis, split_axis=0, concat_axis=0, tiled=True)  59.5 us
    all_to_all x2, waiting for transfers between devices, sent_to_all(): lax.all_to_all(jnp.broadcast_to(x[None], (size, *x.shape)), axis, 0, 0, t...  42.2 us
    dot_general x12, matrix products, update_one_block(): jnp.einsum('gjts,sgd->gjtd', weights.astype(jnp.bfloat16), values_block,...  36.9 us
    all_gather x1, waiting for transfers between devices, in_one_piece(): result = lax.all_gather(both, axis, axis=dim, tiled=True)  35.1 us
    dot_general x12, matrix products, update_one_block(): jnp.einsum('gjtd,sgd->gjts', queries, keys_block, preferred_element_type=...  20.9 us
    add x12, other arithmetic, update_one_block(): totals = totals * factor + jnp.sum(weights, axis=3)  14.8 us
  transfers between devices with their start and end apart: 6, of which 6 were waited for; matrix products, arithmetic and copies ran while one was open for 3% of the time, Pallas kernels for 0%

profile of v1, /device:TPU:0, one launch (start us, length us, event | category | flops | bytes accessed | tf_op | source)
XLA Modules:
  0.0 550.7 jit_solution(15543789882807994988)
XLA Ops:
  6.6 2.0 convert_reduce_fusion
  11.3 2.0 copy.58
  13.3 1.9 slice_bitcast_fusion
  15.2 16.2 %while.28 = (s32[]{:T(128)}, bf16[3,1,256,80]{2,3,1,0:T(8,128)(2,1)}, s32[3]{0:T(128)S(1)}, s32[768]{0:T(1024)S(1)}, bf16[1,768,80]{2,1,0:T(8,128)(2,1)}, /*inde...) while((s32[]{:T(128)}, ...), condition=%wide.region_10.11_spmd, body=%wide.region_7.10_spmd.sunk | while | flops 64527876 | bytes 2797211 | solution.py:84
  32.5 3.5 fusion.81
  36.0 7.2 %all-to-all-start = ((f32[16,48,1280]{2,1,0:T(8,128)}), f32[16,48,1280]{2,1,0:T(8,128)}, u32[]{:S(2)}, u32[]{:S(2)}) async-start(f32[16,48,1280]{2,1,0:T(8,128)} %fusion.81), calls=%async_computation | async-start | bytes 7864320 | tf_op jit(solution)/shard_map/all_to_all | solution.py:21
  43.2 59.5 %all-to-all-done = f32[16,48,1280]{2,1,0:T(8,128)} async-done(((f32[16,48,1280]{2,1,0:T(8,128)}), f32[16,48,1280]{2,1,0:T(8,128)}, u32[]{:S(2)}, u32[]{:S(2)}) %all-to-all-start) | async-done | bytes 3932192 | tf_op jit(solution)/shard_map/all_to_all | solution.py:21
  102.7 2.3 reduce_sum.97
  107.9 4.5 all-to-all-start.1
  115.6 24.9 %all-to-all-done.1 = bf16[16,48,1280]{2,1,0:T(8,128)(2,1)} async-done(((bf16[16,48,1280]{2,1,0:T(8,128)(2,1)}), bf16[16,48,1280]{2,1,0:T(8,128)(2,1)}, u32[]{:S(2)}, u32[]{:S(2)}) %all-to-all-start.1) | async-done | bytes 1966112 | tf_op jit(solution)/shard_map/all_to_all | solution.py:33
  140.5 4.1 reshape_reshape.3
  144.6 3.6 fusion.68
  149.3 5.3 all-to-all-start.2
  154.7 17.3 %all-to-all-done.2 = bf16[8,192,320]{2,1,0:T(8,128)(2,1)S(1)} async-done(((bf16[8,192,320]{2,1,0:T(8,128)(2,1)}), bf16[8,192,320]{2,1,0:T(8,128)(2,1)S(1)}, u32[]{:S(2)}, u32[]{:S(2)}) %all-to-all-start.2) | async-done | bytes 983072 | tf_op jit(solution)/shard_map/all_to_all | solution.py:33
  171.9 11.0 %gather_fusion = bf16[3072,320]{1,0:T(8,128)(2,1)S(1)} fusion(bf16[1536,320]{1,0:T(8,128)(2,1)S(1)} %bitcast.152, s32[3072]{0:T(1024)S(1)} %broadcast_clamp_fusion), kind=kCustom, calls=%fused_computation | custom fusion | bytes 3944448 | tf_op jit(solution)/shard_map/jit(_take)/gather | solution.py:162
  182.9 7.6 %fusion.49 = f32[3072,1024]{1,0:T(8,128)} fusion(bf16[320,1024]{1,0:T(8,128)(2,1)} %param.28, bf16[3072,320]{1,0:T(8,128)(2,1)S(1)} %gather_fusion, pred[3072]{0:T(1024)(128)(4,1)} %compare_and_fusion.1, pred[3072]{0:T(1024)(128)(4,1)S(1)} %ge.77), kind=kOutput, calls=%fused_computation.63 | convolution fusion | flops 2015232000 | bytes 15210496 | tf_op jit(solution)/shard_map/dot_general | solution.py:165
  192.1 88.8 %reduce-scatter.2.cloned.1.call-done = f32[192,1024]{1,0:T(8,128)} async-done(((f32[3072,1024]{1,0:T(8,128)}), f32[192,1024]{1,0:T(8,128)}) %reduce-scatter.2.cloned.1.call-update) | async-done | bytes 786448 | tf_op jit(solution)/shard_map/reduce_scatter | solution.py:164
  282.1 2.1 gather_fusion.1
  284.7 9.6 %all_to_all.27 = f32[8,1,384]{2,1,0:T(1,128)S(1)} all-to-all(f32[8,1,384]{2,1,0:T(1,128)S(1)} %broadcast_in_dim.162), channel_id=1, replica_groups=mesh['enc'=8,'ctx'=16] {'enc'}, dimensions={0} | all-to-all | bytes 24576 | tf_op jit(solution)/shard_map/all_to_all | solution.py:33
  294.3 3.5 tile.2
  297.8 4.7 all-to-all-start.3
  302.6 72.0 %all-to-all-done.3 = bf16[384,8,1024]{2,0,1:T(8,128)(2,1)} async-done(((bf16[384,8,1024]{2,0,1:T(8,128)(2,1)}), bf16[384,8,1024]{2,0,1:T(8,128)(2,1)}, u32[]{:S(2)}, u32[]{:S(2)}) %all-to-all-start.3) | async-done | bytes 6291488 | tf_op jit(solution)/shard_map/all_to_all | solution.py:111
  374.6 8.6 %copy.60 = bf16[384,8,1024]{0,2,1:T(8,128)(2,1)} copy(bf16[384,8,1024]{2,0,1:T(8,128)(2,1)} %all-to-all-done.3) | data formatting | bytes 12582912 | tf_op jit(solution)/shard_map/all_to_all | solution.py:111
  383.3 5.6 %fusion.42 = bf16[384,8192]{0,1:T(8,128)(2,1)S(1)} fusion(bf16[384,8,1024]{0,2,1:T(8,128)(2,1)} %copy.60, f32[8192]{0:T(1024)S(1)} %copy-done.6, f32[384]{0:T(512)S(1)} %add_rsqrt_fusion.1), kind=kLoop, calls=%fused_computation.52 | loop fusion | flops 12582912 | bytes 12617216 | tf_op jit(solution)/shard_map/convert_element_type | solution.py:183
  398.1 8.8 %convolution_convert_fusion = bf16[384,512]{1,0:T(8,128)(2,1)S(1)} fusion(bf16[384,8192]{0,1:T(8,128)(2,1)} %copy-done.2, bf16[8192,512]{1,0:T(8,128)(2,1)} %param.33), kind=kOutput, calls=%fused_computation.73 | convolution fusion | flops 3221422080 | bytes 15073280 | tf_op jit(solution)/shard_map/dot_general | solution.py:184
  407.8 35.1 %all-gather.2.cloned.1.call-done = bf16[6144,256]{0,1:T(8,128)(2,1)} async-done(((bf16[384,256]{0,1:T(8,128)(2,1)}), bf16[6144,256]{0,1:T(8,128)(2,1)}) %all-gather.2.cloned.1.call-update) | async-done | bytes 3145744 | tf_op jit(solution)/shard_map/all_gather | solution.py:47
  442.9 98.2 %conditional.1 = (f32[1,4,384]{2,1,0:T(4,128)}, f32[1,4,384,128]{3,2,1,0:T(8,128)}) conditional(s32[]{:T(128)} %convert_element_type.78, () %tuple.31, (bf16[6144,256]{0,1:T(8,128)(2,1)}, s32[]{:T(128)}, s32[384]{0:T(512)S(1)}, s32[6144]{0:T(1024)}, s32[384]{0:T(512)S(1)}, /*index=5*/bf16[1,4,384,128]{3,2,1,0:T(8,128)(2,1)}) %tuple.87), branch_computations={%region_17.18_spmd, %region_18.23_spmd} | conditional | flops 412493696 | bytes 25149788 | solution.py:247
  442.9 3.2 copy.63
  446.1 1.9 fusion.89
  448.0 93.2 %while.27 = (s32[]{:T(128)}, f32[1,4,384]{2,1,0:T(4,128)S(1)}, f32[1,4,384]{2,1,0:T(4,128)}, f32[1,4,384,128]{3,2,1,0:T(8,128)}, s32[384]{0:T(512)S(1)}, /*index...) while((s32[]{:T(128)}, f32[1,4,384]{2,1,0:T(4,128)S(1)}, ...), condition=%wide.region_22.22_spmd.clone, body=%wide.region_19.21_spmd.clone.sunk | while | flops 412493312 | bytes 12563663 | solution.py:242
  450.7 2.8 fusion.121
  457.6 3.1 fusion.121
  463.7 1.7 fusion.118
  465.4 3.1 fusion.121
  471.5 1.7 fusion.118
  473.3 3.1 fusion.121
  479.4 1.7 fusion.118
  481.1 3.1 fusion.121
  487.2 1.7 fusion.118
  489.0 3.1 fusion.121
  495.1 1.7 fusion.118
  496.8 3.1 fusion.121
  502.9 1.7 fusion.118
  504.7 3.1 fusion.121
  512.5 3.1 fusion.121
  520.4 3.1 fusion.121
  528.2 3.1 fusion.121
  536.1 3.1 fusion.121
  (199 shorter events, 81.0 us)
Async XLA Ops:
  6.5 138.1 %copy-start = (bf16[5120,320]{0,1:T(8,128)(2,1)S(1)}, bf16[5120,320]{0,1:T(8,128)(2,1)}, u32[]{:S(2)}) copy-start(bf16[5120,320]{0,1:T(8,128)(2,1)} %param.27) | copy-start | bytes 9830404
  6.5 3.0 copy-start.12
  6.5 2.3 copy-start.3
  6.5 3.0 copy-start.11
  9.5 5.7 %copy-start.8 = (s32[768]{0:T(1024)S(1)}, s32[768]{0:T(1024)}, u32[]{:S(2)}) copy-start(s32[768]{0:T(1024)} %param.22) | copy-start | bytes 9220
  36.0 66.7 %all-to-all-start = ((f32[16,48,1280]{2,1,0:T(8,128)}), f32[16,48,1280]{2,1,0:T(8,128)}, u32[]{:S(2)}, u32[]{:S(2)}) async-start(f32[16,48,1280]{2,1,0:T(8,128)} %fusion.81), calls=%async_computation | async-start | bytes 7864320 | tf_op jit(solution)/shard_map/all_to_all | solution.py:21
  43.2 63.2 %copy-start.7 = (f32[1280]{0:T(1024)S(1)}, f32[1280]{0:T(1024)}, u32[]{:S(2)}) copy-start(f32[1280]{0:T(1024)} %param.26) | copy-start | bytes 15364
  106.3 6.0 %copy-start.5 = (s32[6144]{0:T(1024)S(1)}, s32[6144]{0:T(1024)}, u32[]{:S(2)}) copy-start(s32[6144]{0:T(1024)} %param.30) | copy-start | bytes 73732
  107.9 32.7 %all-to-all-start.1 = ((bf16[16,48,1280]{2,1,0:T(8,128)(2,1)}), bf16[16,48,1280]{2,1,0:T(8,128)(2,1)}, u32[]{:S(2)}, u32[]{:S(2)}) async-start(bf16[16,48,1280]{2,1,0:T(8,128)(2,1)} %broadcast_in_dim.157), calls=%async_computation.1 | async-start | bytes 3932160 | tf_op jit(solution)/shard_map/all_to_all | solution.py:33
  149.3 22.6 %all-to-all-start.2 = ((bf16[8,192,320]{2,1,0:T(8,128)(2,1)}), bf16[8,192,320]{2,1,0:T(8,128)(2,1)S(1)}, u32[]{:S(2)}, u32[]{:S(2)}) async-start(bf16[8,192,320]{2,1,0:T(8,128)(2,1)} %broadcast_in_dim.158), calls=%async_computation.2 | async-start | bytes 2359296 | tf_op jit(solution)/shard_map/all_to_all | solution.py:33
  154.6 126.3 %reduce-scatter.2.cloned.1.call-start = ((), (), s32[]{:S(2)}) async-start(), calls=%async_computation.6 | async-start | bytes 13369344 | tf_op jit(solution)/shard_map/reduce_scatter | solution.py:164
  282.1 2.1 copy-start.4
  297.8 76.9 %all-to-all-start.3 = ((bf16[384,8,1024]{2,0,1:T(8,128)(2,1)}), bf16[384,8,1024]{2,0,1:T(8,128)(2,1)}, u32[]{:S(2)}, u32[]{:S(2)}) async-start(bf16[384,8,1024]{2,0,1:T(8,128)(2,1)} %tile.2), calls=%async_computation.4 | async-start | bytes 12582912 | tf_op jit(solution)/shard_map/all_to_all | solution.py:111
  302.5 140.4 %all-gather.2.cloned.1.call-start = ((), (), s32[]{:S(2)}) async-start(), calls=%async_computation.7 | async-start | bytes 3342336 | tf_op jit(solution)/shard_map/all_gather | solution.py:47
  302.6 80.6 %copy-start.6 = (f32[8192]{0:T(1024)S(1)}, f32[8192]{0:T(1024)}, u32[]{:S(2)}) copy-start(f32[8192]{0:T(1024)} %param.32) | copy-start | bytes 98308
  383.3 5.6 %copy-start.9 = (bf16[8192,128]{1,0:T(8,128)(2,1)S(1)}, bf16[8192,128]{1,0:T(8,128)(2,1)}, u32[]{:S(2)}) copy-start(bf16[8192,128]{1,0:T(8,128)(2,1)} %param.35) | copy-start | bytes 6291460
  388.9 2.9 copy-start.2
  388.9 3.2 copy-start.10
  541.2 2.7 copy-start.1
Sparse Core Ops, SparseCore 0:
  190.7 90.1 reduce-scatter.1
  394.2 48.6 all-gather.1
